TPU v7x, 256 devices: a whole 4x4x8 slice. The times are simulated.
256 devices in a mesh: dp: 16 (over y, x_hi, core), tensor: 16 (over x_lo, z).
Axes of the slice: x: 4 (x_hi: 2, x_lo: 2; x = x_hi * 2 + x_lo), y: 4, z: 8, core: 2. Of those that a mesh axis runs over, the one named last changes fastest.
Arguments:
- h_values: bfloat16 [12288, 16384], P(('dp', 'tensor')), may hold values from -448 to 448
- h_scales: bfloat16 [12288, 128], P(('dp', 'tensor')), may hold values from 0.00049972534 to 0.0099487305
- dy_values: bfloat16 [12288, 4096], P(('dp', 'tensor')), may hold values from -448 to 448
- dy_scales: bfloat16 [12288, 32], P(('dp', 'tensor')), may hold values from 1.9907951e-05 to 0.00039863586
Outputs:
- grad_down: bfloat16 [4096, 16384], P('dp', 'tensor')
All inputs are finite; a program needn't handle non-finite values.
Results may differ from a plain program's by a relative error of at most 0.02.
Values may be sent and summed in bfloat16 or wider, within the bound.
A program may use at most 192 MiB of HBM per device.

v0:
```python
import jax
import jax.numpy as jnp
from jax import lax
from jax.sharding import PartitionSpec as P

QBLOCK = 128


def dequantize(values, scales):
    row_count, col_count = values.shape
    block_total = scales.shape[1]
    widened = values.astype(jnp.float32).reshape(row_count, block_total, col_count // block_total)
    widened = widened * scales.astype(jnp.float32)[:, :, None]
    return widened.reshape(row_count, col_count)


def requantize(field):
    row_count, col_count = field.shape
    blocked = field.reshape(row_count // QBLOCK, QBLOCK, col_count)
    largest = jnp.max(jnp.abs(blocked), axis=1)
    column_scale = ((largest + 1e-06) / 448.0).astype(jnp.bfloat16)
    quantized = (blocked / column_scale.astype(jnp.float32)[:, None, :]).astype(jnp.bfloat16)
    return (quantized.reshape(row_count, col_count), column_scale)


def group_product(grad_q, grad_scale, hidden_q, hidden_scale):
    block_count = grad_q.shape[0] // QBLOCK
    summed = jnp.zeros((grad_q.shape[1], hidden_q.shape[1]), jnp.float32)
    for block_index in range(block_count):
        grad_block = grad_q[block_index * QBLOCK : (block_index + 1) * QBLOCK]
        hidden_block = hidden_q[block_index * QBLOCK : (block_index + 1) * QBLOCK]
        product = lax.dot_general(
            grad_block, hidden_block, (((0,), (0,)), ((), ())), preferred_element_type=jnp.float32
        )
        row_factor = grad_scale[block_index].astype(jnp.float32)[:, None]
        col_factor = hidden_scale[block_index].astype(jnp.float32)[None, :]
        summed = summed + product * row_factor * col_factor
    return summed


def shards(h_values, h_scales, dy_values, dy_scales):
    hidden_vals, hidden_blocks = (
        lax.all_to_all(h_values, "tensor", split_axis=1, concat_axis=0, tiled=True),
        lax.all_to_all(h_scales, "tensor", split_axis=1, concat_axis=0, tiled=True),
    )
    grad_vals, grad_blocks = (
        lax.all_gather(dy_values, "tensor", axis=0, tiled=True),
        lax.all_gather(dy_scales, "tensor", axis=0, tiled=True),
    )
    hidden_q, hidden_scale = requantize(dequantize(hidden_vals, hidden_blocks))
    grad_q, grad_scale = requantize(dequantize(grad_vals, grad_blocks))
    return lax.psum_scatter(
        group_product(grad_q, grad_scale, hidden_q, hidden_scale).astype(jnp.bfloat16),
        "dp",
        scatter_dimension=0,
        tiled=True,
    )


def solution(mesh):
    placed = (
        P(("dp", "tensor"), None),
        P(("dp", "tensor"), None),
        P(("dp", "tensor"), None),
        P(("dp", "tensor"), None),
    )
    return jax.shard_map(
        shards, mesh=mesh, in_specs=placed, out_specs=P("dp", "tensor"), check_vma=False
    )
```

profile of v0, /device:TPU:2, one launch (start us, length us, event | category | flops | bytes accessed | tf_op | source)
XLA Modules:
  0.0 343.9 jit_solution(2101893840816630577)
XLA Ops:
  6.5 0.0 all-gather.3.cloned.1.call-start
  6.5 0.7 all-gather.3.cloned.1.call-update
  7.3 0.8 copy.19
  8.1 0.7 reshape.117
  8.8 9.9 %all-to-all-start.1 = ((bf16[16,2,192]{2,1,0:T(2,128)(2,1)}), bf16[16,2,192]{2,1,0:T(2,128)(2,1)S(1)}, u32[]{:S(2)}, u32[]{:S(2)}) async-start(bf16[16,2,192]{2,1,0:T(2,128)(2,1)} %reshape.117), calls=%async_computation.1 | async-start | bytes 32768 | tf_op jit(solution)/shard_map/all_to_all | solution.py:44
  18.7 2.7 copy.28
  21.5 4.5 %all-to-all-done.1 = bf16[16,2,192]{2,1,0:T(2,128)(2,1)S(1)} async-done(((bf16[16,2,192]{2,1,0:T(2,128)(2,1)}), bf16[16,2,192]{2,1,0:T(2,128)(2,1)S(1)}, u32[]{:S(2)}, u32[]{:S(2)}) %all-to-all-start.1) | async-done | bytes 12320 | tf_op jit(solution)/shard_map/all_to_all | solution.py:44
  25.9 5.6 %all-to-all-start = ((bf16[48,16,1024]{2,0,1:T(8,128)(2,1)}), bf16[48,16,1024]{2,0,1:T(8,128)(2,1)}, u32[]{:S(2)}, u32[]{:S(2)}) async-start(bf16[48,16,1024]{2,0,1:T(8,128)(2,1)} %bitcast.67), calls=%async_computation | async-start | bytes 3145728 | tf_op jit(solution)/shard_map/all_to_all | solution.py:43
  31.5 0.0 reduce-scatter.2.cloned.1.call-start
  31.6 80.1 %all-gather = bf16[16,48,32]{1,2,0:T(8,128)(2,1)S(1)} all-gather(bf16[1,48,32]{1,2,0:T(8,128)(2,1)} %bitcast.80), channel_id=1, replica_groups=mesh['dp'=16,'tensor'=16] {'tensor'}, dimensions={0}, use_global_device_ids=true | all-gather | bytes 52224 | tf_op jit(solution)/shard_map/all_gather | solution.py:48
  111.7 0.1 copy.22
  111.8 7.1 %mul.148 = f32[768,32,128]{2,1,0:T(8,128)} broadcast(f32[768,32]{1,0:T(8,128)S(1)} %bitcast.71), dimensions={0,1} | broadcast | bytes 12681216 | tf_op jit(solution)/shard_map/mul | solution.py:13
  118.9 13.8 %mul.149 = f32[6,128,4096]{2,1,0:T(8,128)} reshape(f32[768,32,128]{2,1,0:T(8,128)} %mul.148) | data formatting | bytes 25165824 | tf_op jit(solution)/shard_map/mul | solution.py:13
  132.7 0.1 reshape.118
  132.8 0.2 copy.23
  133.0 0.9 mul.151
  133.9 2.4 mul.152
  136.2 0.0 all-to-all-done
  136.2 1.8 convert_element_type.171
  138.0 2.6 abs_reduce_fusion.1
  140.7 0.5 divide_convert_fusion.1
  141.2 0.0 all-gather.3.cloned.1.call-done
  141.2 8.5 %abs_reduce_fusion = f32[6,4096]{1,0:T(8,128)S(1)} fusion(f32[6,128,4096]{2,1,0:T(8,128)} %mul.149, bf16[6,128,4096]{2,1,0:T(8,128)(2,1)} %bitcast.68), kind=kLoop, calls=%fused_computation.3 | loop fusion | flops 12558336 | bytes 18972672 | tf_op jit(solution)/shard_map/reduce_max | solution.py:20
  149.8 7.6 %divide_convert_fusion = bf16[6,128,4096]{2,1,0:T(8,128)(2,1)S(1)} fusion(f32[6,128,4096]{2,1,0:T(8,128)} %mul.149, bf16[6,128,4096]{2,1,0:T(8,128)(2,1)} %bitcast.69, f32[6,4096]{1,0:T(8,128)S(1)} %get-tuple-element.9), kind=kLoop, calls=%fused_computation.2 | loop fusion | flops 12582912 | bytes 25264128 | tf_op jit(solution)/shard_map/convert_element_type | solution.py:22
  157.4 0.0 copy-start
  157.4 8.1 %fusion = f32[4096,1024]{1,0:T(8,128)} fusion(bf16[6,128,4096]{2,1,0:T(8,128)(2,1)S(1)} %divide_convert_fusion, bf16[6,128,1024]{2,1,0:T(8,128)(2,1)S(1)} %divide_convert_fusion.1), kind=kOutput, calls=%fused_computation.9 | convolution fusion | flops 1073741824 | bytes 18087936 | tf_op jit(solution)/shard_map/dot_general | solution.py:32
  165.5 8.1 %fusion.1 = f32[4096,1024]{1,0:T(8,128)} fusion(bf16[6,128,4096]{2,1,0:T(8,128)(2,1)S(1)} %divide_convert_fusion, bf16[6,128,1024]{2,1,0:T(8,128)(2,1)S(1)} %divide_convert_fusion.1), kind=kOutput, calls=%fused_computation.11 | convolution fusion | flops 1073741824 | bytes 18087936 | tf_op jit(solution)/shard_map/dot_general | solution.py:32
  173.6 8.1 %fusion.2 = f32[4096,1024]{1,0:T(8,128)} fusion(bf16[6,128,4096]{2,1,0:T(8,128)(2,1)S(1)} %divide_convert_fusion, bf16[6,128,1024]{2,1,0:T(8,128)(2,1)S(1)} %divide_convert_fusion.1), kind=kOutput, calls=%fused_computation.13 | convolution fusion | flops 1073741824 | bytes 18087936 | tf_op jit(solution)/shard_map/dot_general | solution.py:32
  181.6 8.1 %fusion.3 = f32[4096,1024]{1,0:T(8,128)} fusion(bf16[6,128,4096]{2,1,0:T(8,128)(2,1)S(1)} %divide_convert_fusion, bf16[6,128,1024]{2,1,0:T(8,128)(2,1)S(1)} %divide_convert_fusion.1), kind=kOutput, calls=%fused_computation.15 | convolution fusion | flops 1073741824 | bytes 18087936 | tf_op jit(solution)/shard_map/dot_general | solution.py:32
  189.7 0.0 copy-done
  189.7 8.2 %fusion.4 = f32[4096,1024]{1,0:T(8,128)} fusion(bf16[6,128,4096]{2,1,0:T(8,128)(2,1)S(1)} %divide_convert_fusion, bf16[6,128,1024]{2,1,0:T(8,128)(2,1)S(1)} %divide_convert_fusion.1), kind=kOutput, calls=%fused_computation.17 | convolution fusion | flops 1073741824 | bytes 18087936 | tf_op jit(solution)/shard_map/dot_general | solution.py:32
  197.9 0.1 slice_convert_fusion.5
  198.0 32.2 %add_convert_fusion = bf16[4096,1024]{1,0:T(8,128)(2,1)} fusion(f32[4096,1024]{1,0:T(8,128)} %fusion, f32[4096,1024]{1,0:T(8,128)} %fusion.1, f32[4096,1024]{1,0:T(8,128)} %fusion.2, f32[4096,1024]{1,0:T(8,128)} %fusion.3, f32[4096,1024]{1,0:T(8,128)} %fusion.4, f32[1024]{0:T(1024)S(1)} %bitcast.86, f32[4096]{0:T(1024)S(1)} %bitcast.79, ...), kind=kOutput, calls=%fused_computation | convolution fusion | flops 1149239296 | bytes 93708288 | tf_op jit(solution)/shard_map/dot_general | solution.py:32
  230.2 0.0 reduce-scatter.2.cloned.1.call-update
  230.2 106.8 %reduce-scatter.2.cloned.1.call-done = bf16[256,1024]{1,0:T(8,128)(2,1)} async-done(((bf16[4096,1024]{1,0:T(8,128)(2,1)}), bf16[256,1024]{1,0:T(8,128)(2,1)}) %reduce-scatter.2.cloned.1.call-update) | async-done | bytes 524304 | tf_op jit(solution)/shard_map/reduce_scatter | solution.py:52
  (5 shorter events, 0.1 us)
Async XLA Ops:
  6.5 134.7 %all-gather.3.cloned.1.call-start = ((), (), s32[]{:S(2)}) async-start(), calls=%async_computation.3 | async-start | bytes 6684672 | tf_op jit(solution)/shard_map/all_gather | solution.py:47
  8.8 17.1 %all-to-all-start.1 = ((bf16[16,2,192]{2,1,0:T(2,128)(2,1)}), bf16[16,2,192]{2,1,0:T(2,128)(2,1)S(1)}, u32[]{:S(2)}, u32[]{:S(2)}) async-start(bf16[16,2,192]{2,1,0:T(2,128)(2,1)} %reshape.117), calls=%async_computation.1 | async-start | bytes 32768 | tf_op jit(solution)/shard_map/all_to_all | solution.py:44
  25.9 110.3 %all-to-all-start = ((bf16[48,16,1024]{2,0,1:T(8,128)(2,1)}), bf16[48,16,1024]{2,0,1:T(8,128)(2,1)}, u32[]{:S(2)}, u32[]{:S(2)}) async-start(bf16[48,16,1024]{2,0,1:T(8,128)(2,1)} %bitcast.67), calls=%async_computation | async-start | bytes 3145728 | tf_op jit(solution)/shard_map/all_to_all | solution.py:43
  31.5 305.5 %reduce-scatter.2.cloned.1.call-start = ((), (), s32[]{:S(2)}) async-start(), calls=%async_computation.4 | async-start | bytes 8912896 | tf_op jit(solution)/shard_map/reduce_scatter | solution.py:52
  157.4 32.4 %copy-start = (bf16[6,128,4096]{2,1,0:T(8,128)(2,1)}, bf16[6,128,4096]{2,1,0:T(8,128)(2,1)S(1)}, u32[]{:S(2)}) copy-start(bf16[6,128,4096]{2,1,0:T(8,128)(2,1)S(1)} %divide_convert_fusion) | copy-start | bytes 18874372
Sparse Core Ops, SparseCore 0:
  9.1 119.1 all-gather.2
  230.3 106.6 reduce-scatter.1
where the time goes:
time: 345 us; the launch traced here: 344 us
  waiting for transfers between devices  112 us (32%)
  blocking collectives  80.1 us (23%)
  matrix products  72.7 us (21%)
  local copies, waits for them, and re-layouts  28.8 us (8%)
  other arithmetic  21.1 us (6%)
  starting transfers between devices  15.6 us (5%)
  between operations  13.5 us (4%)
    reduce_scatter x1, waiting for transfers between devices, shards(): lax.psum_scatter(group_product(grad_q, grad_scale, hidden_q, hidden_scale...  107 us
    all_gather x1, blocking collectives, shards(): lax.all_gather(dy_scales, 'tensor', axis=0, tiled=True)  80.1 us
    dot_general x6, matrix products, group_product(): lax.dot_general(grad_block, hidden_block, (((0,), (0,)), ((), ())), prefe...  72.7 us
    mul x4, local copies, waits for them, and re-layouts, dequantize(): widened = widened * scales.astype(jnp.float32)[:, :, None]  24.1 us
    reduce_max x2, other arithmetic, requantize(): largest = jnp.max(jnp.abs(blocked), axis=1)  11.1 us
    all_to_all x1, starting transfers between devices, shards(): lax.all_to_all(h_scales, 'tensor', split_axis=1, concat_axis=0, tiled=True)  9.94 us
    convert_element_type x2, other arithmetic, requantize(): (blocked / column_scale.astype(jnp.float32)[:, None, :]).astype(jnp.bfloa...  8.04 us
  transfers between devices with their start and end apart: 4, of which 2 were waited for; matrix products, arithmetic and copies ran while one was open for 10% of the time, Pallas kernels for 0%

commit v1 on v0

v1 whole, which is shorter than its diff:
```python
import jax
import jax.numpy as jnp
from jax import lax
from jax.experimental import pallas as pl
from jax.experimental.pallas import tpu as pltpu
from jax.sharding import PartitionSpec as P

QBLOCK = 128
MESH = pl.DeviceIdType.MESH
XN, YN, ZN = 4, 4, 8
TOK = 48
LINE = ZN * TOK
KTOK = XN * LINE
ROWS = 1024
HALF = ROWS // 2
COLS = 2048
NCH = 4
W = COLS // NCH
F32, BF16 = jnp.float32, jnp.bfloat16


def requantize(block):
    largest = jnp.max(jnp.abs(block), axis=0, keepdims=True)
    scale = ((largest + 1e-6) / 448.0).astype(BF16).astype(F32)
    quantized = (block * (1.0 / scale)).astype(BF16).astype(F32)
    return quantized * scale


def kernel(hv, hs, dv, ds, out,
           dyp, gat, hsend, hz, hx, gt, px, pr, po,
           sp, sm, rp, rm, cp, cm, qp, qm, fb, fr,
           hss, hrs, dxs, dxr, dzs, dzr, xss, xrs, xfs, xfr, cs, cr, ys, yr, fs, frs):
    dp, t = lax.axis_index("dp"), lax.axis_index("tensor")
    c, xh, y = dp % 2, (dp // 2) % 2, dp // 4
    xl, z = t // 8, t % 8
    x = xh * 2 + xl

    def dev(x_=None, y_=None, z_=None, c_=None):
        x_ = x if x_ is None else x_
        y_ = y if y_ is None else y_
        z_ = z if z_ is None else z_
        c_ = c if c_ is None else c_
        return ((y_ * 2 + x_ // 2) * 2 + c_, (x_ % 2) * 8 + z_)

    def send(src, dst, ssem, rsem, to):
        return pltpu.make_async_remote_copy(
            src_ref=src, dst_ref=dst, send_sem=ssem, recv_sem=rsem, device_id=to, device_id_type=MESH)

    def zrow(zs):
        return pl.ds(pl.multiple_of(zs * TOK, 16), TOK)

    def xrow(xs, lo=0, n=LINE):
        return pl.ds(pl.multiple_of(xs * LINE + lo, 16), n)

    barrier = pltpu.get_barrier_semaphore()
    peers = ([dev(x_=(x + d) % XN) for d in range(1, XN)] + [dev(y_=(y + d) % YN) for d in (1, 3)]
             + [dev(z_=(z + d) % ZN) for d in range(1, ZN)] + [dev(c_=1 - c)])
    for peer in peers:
        pl.semaphore_signal(barrier, inc=1, device_id=peer, device_id_type=MESH)

    for j in range(32):
        y_, a_, c_, b_ = j // 8, (j // 4) % 2, (j // 2) % 2, j % 2
        q = c_ * YN + y_
        val = dv[:, j * 128:(j + 1) * 128].astype(F32) * ds[:, j:j + 1].astype(F32)
        dyp[a_ * 2 + b_, :, q * 128:(q + 1) * 128] = val.astype(BF16)
    gat[x, zrow(z), :] = dyp[x]

    pl.semaphore_wait(barrier, len(peers))

    dx = []
    for d in range(1, XN):
        to = (x + d) % XN
        cpy = send(dyp.at[to], gat.at[x, zrow(z)], dxs.at[d - 1], dxr.at[d - 1], dev(x_=to))
        cpy.start()
        dx.append(cpy)

    hcp = []
    blocks = W // 128
    for k in range(NCH):
        for zz in range(ZN):
            for i in range(blocks):
                col = k * W + i * 128
                j = ((col // 1024) * 8 + zz) * 8 + (col % 1024) // 128
                val = hv[:, j * 128:(j + 1) * 128].astype(F32) * hs[:, j:j + 1].astype(F32)
                hsend[k, zz, :, i * 128:(i + 1) * 128] = val.astype(BF16)
        row = []
        for n, d in enumerate((1, 7, 2, 6, 3, 5, 4)):
            to = (z + d) % ZN
            cpy = send(hsend.at[k, to], hz.at[k, zrow(z)], hss.at[k, n], hrs.at[k, n], dev(z_=to))
            cpy.start()
            row.append(cpy)
        hcp.append(row)
        hz[k, zrow(z), :] = hsend[k, z]

    zu, zd = dev(z_=(z + 1) % ZN), dev(z_=(z + 7) % ZN)

    def ring(s):
        su, sd = (z + 8 - s) % ZN, (z + s) % ZN
        if s < 3:
            up, dn = gat.at[:, zrow(su)], gat.at[:, zrow(sd)]
        else:
            up, dn = gat.at[0:2, zrow(su)], gat.at[2:4, zrow(sd)]
        return (send(up, up, dzs.at[0, s], dzr.at[0, s], zu), send(dn, dn, dzs.at[1, s], dzr.at[1, s], zd))

    rings = [ring(s) for s in range(4)]
    for cpy in dx:
        cpy.wait_recv()
    for cpy in rings[0]:
        cpy.start()

    xu, xd = dev(x_=(x + 1) % XN), dev(x_=(x + 3) % XN)
    xup, xdn = (x + 3) % XN, (x + 1) % XN
    xcp, fcp = [], []

    def forward(k):
        for cpy in xcp[k]:
            cpy.wait_recv()
        up, dn = hx.at[k, xrow(xup, 0, LINE // 2)], hx.at[k, xrow(xdn, LINE // 2, LINE // 2)]
        pair = (send(up, up, xfs.at[k, 0], xfr.at[k, 0], xu), send(dn, dn, xfs.at[k, 1], xfr.at[k, 1], xd))
        for cpy in pair:
            cpy.start()
        fcp.append(pair)

    for k in range(NCH):
        for cpy in hcp[k]:
            cpy.wait_recv()

        @pl.loop(0, W // 128)
        def _(i):
            lanes = pl.ds(pl.multiple_of(i * 128, 128), 128)
            for b in range(LINE // QBLOCK):
                val = requantize(hz[k, b * QBLOCK:(b + 1) * QBLOCK, lanes].astype(F32))
                hx[k, xrow(x, b * QBLOCK, QBLOCK), lanes] = val.astype(BF16)

        mine = hx.at[k, xrow(x)]
        pair = (send(mine, mine, xss.at[k, 0], xrs.at[k, 0], xu), send(mine, mine, xss.at[k, 1], xrs.at[k, 1], xd))
        for cpy in pair:
            cpy.start()
        xcp.append(pair)
        if k:
            forward(k - 1)
    forward(NCH - 1)

    for s in range(4):
        for cpy in rings[s]:
            cpy.wait_recv()
        if s < 3:
            for cpy in rings[s + 1]:
                cpy.start()

    for b in range(KTOK // QBLOCK):
        xs, bb = b // 3, b % 3

        @pl.loop(0, ROWS // 128)
        def _(i):
            at = pl.ds(pl.multiple_of(i * 128, 128), 128)
            val = requantize(gat[xs, bb * QBLOCK:(bb + 1) * QBLOCK, at].astype(F32))
            gt[at, b * QBLOCK:(b + 1) * QBLOCK] = val.T.astype(BF16)

    partner = dev(c_=1 - c)
    yu, yd = dev(y_=(y + 1) % YN), dev(y_=(y + 3) % YN)
    core_cp, ring_cp, tail_cp = [], [], []

    def product(k):
        for cpy in fcp[k]:
            cpy.wait_recv()

        @pl.loop(0, 2)
        def _(i):
            rows = pl.ds(pl.multiple_of((1 - c) * HALF + i * 256, 256), 256)
            at = pl.ds(pl.multiple_of(i * 256, 256), 256)
            px[k, at, :] = jnp.dot(gt[rows, :], hx[k], preferred_element_type=F32).astype(BF16)

        cpy = send(px.at[k], pr.at[k], cs.at[k], cr.at[k], partner)
        cpy.start()
        core_cp.append(cpy)

        @pl.loop(0, 2)
        def _(i):
            rows = pl.ds(pl.multiple_of(c * HALF + i * 256, 256), 256)
            at = pl.ds(pl.multiple_of(i * 256, 256), 256)
            po[k, at, :] = jnp.dot(gt[rows, :], hx[k], preferred_element_type=F32)

    def part(k, yy, lo):
        return po[k, pl.ds(pl.multiple_of(yy * 128 + lo, 64), 64), :]

    y1, y2, y3 = (y + 1) % YN, (y + 2) % YN, (y + 3) % YN

    def reduce_first(k):
        core_cp[k].wait_recv()
        po[k] = po[k] + pr[k].astype(F32)
        sp[k, 0] = part(k, y2, 0).astype(BF16)
        sp[k, 1] = part(k, y1, 64).astype(BF16)
        sm[k, 0] = part(k, y2, 64).astype(BF16)
        sm[k, 1] = part(k, y3, 0).astype(BF16)
        pair = (send(sp.at[k], rp.at[k], ys.at[k, 0], yr.at[k, 0], yu),
                send(sm.at[k], rm.at[k], ys.at[k, 1], yr.at[k, 1], yd))
        for cpy in pair:
            cpy.start()
        ring_cp.append(pair)

    def reduce_second(k):
        for cpy in ring_cp[k]:
            cpy.wait_recv()
        cp[k] = (part(k, y1, 0) + rp[k, 0].astype(F32)).astype(BF16)
        cm[k] = (part(k, y3, 64) + rm[k, 0].astype(F32)).astype(BF16)
        pair = (send(cp.at[k], qp.at[k], ys.at[k, 2], yr.at[k, 2], yu),
                send(cm.at[k], qm.at[k], ys.at[k, 3], yr.at[k, 3], yd))
        for cpy in pair:
            cpy.start()
        tail_cp.append(pair)

    across = dev(x_=xh * 2 + 1 - xl)
    per = NCH // 2

    def swap(j, k):
        return send(fb.at[k], fr.at[j], fs.at[j], frs.at[j], across)

    def finish(k):
        for cpy in tail_cp[k]:
            cpy.wait_recv()
        fb[k, 0:64] = (part(k, y, 0) + qp[k].astype(F32) + rm[k, 1].astype(F32)).astype(BF16)
        fb[k, 64:128] = (part(k, y, 64) + qm[k].astype(F32) + rp[k, 1].astype(F32)).astype(BF16)

        @pl.when(xl != k // per)
        def _():
            swap(k % per, k).start()

    for k in range(NCH + 3):
        if k < NCH:
            product(k)
        if 0 <= k - 1 < NCH:
            reduce_first(k - 1)
        if 0 <= k - 2 < NCH:
            reduce_second(k - 2)
        if 0 <= k - 3 < NCH:
            finish(k - 3)

    mine_rows = pl.ds(pl.multiple_of(xl * 128, 128), 128)
    other_rows = pl.ds(pl.multiple_of((1 - xl) * 128, 128), 128)
    for j in range(per):
        out[mine_rows, j * W:(j + 1) * W] = fb[xl * per + j]
    for j in range(per):
        swap(j, (1 - xl) * per + j).wait()
        out[other_rows, j * W:(j + 1) * W] = fr[j]

    for group in hcp + [dx] + rings + xcp + fcp + [core_cp] + ring_cp + tail_cp:
        for cpy in group:
            cpy.wait_send()


def shards(h_values, h_scales, dy_values, dy_scales):
    vmem = pl.BlockSpec(memory_space=pltpu.VMEM)
    dma = pltpu.SemaphoreType.DMA
    return pl.pallas_call(
        kernel,
        out_shape=jax.ShapeDtypeStruct((256, 1024), BF16),
        in_specs=[vmem] * 4,
        out_specs=vmem,
        scratch_shapes=[
            pltpu.VMEM((XN, TOK, ROWS), BF16),
            pltpu.VMEM((XN, LINE, ROWS), BF16),
            pltpu.VMEM((NCH, ZN, TOK, W), BF16),
            pltpu.VMEM((NCH, LINE, W), BF16),
            pltpu.VMEM((NCH, KTOK, W), BF16),
            pltpu.VMEM((ROWS, KTOK), BF16),
            pltpu.VMEM((NCH, HALF, W), BF16),
            pltpu.VMEM((NCH, HALF, W), BF16),
            pltpu.VMEM((NCH, HALF, W), F32),
            pltpu.VMEM((NCH, 2, 64, W), BF16),
            pltpu.VMEM((NCH, 2, 64, W), BF16),
            pltpu.VMEM((NCH, 2, 64, W), BF16),
            pltpu.VMEM((NCH, 2, 64, W), BF16),
            pltpu.VMEM((NCH, 64, W), BF16),
            pltpu.VMEM((NCH, 64, W), BF16),
            pltpu.VMEM((NCH, 64, W), BF16),
            pltpu.VMEM((NCH, 64, W), BF16),
            pltpu.VMEM((NCH, 128, W), BF16),
            pltpu.VMEM((NCH // 2, 128, W), BF16),
            dma((NCH, 7)), dma((NCH, 7)),
            dma((3,)), dma((3,)),
            dma((2, 4)), dma((2, 4)),
            dma((NCH, 2)), dma((NCH, 2)),
            dma((NCH, 2)), dma((NCH, 2)),
            dma((NCH,)), dma((NCH,)),
            dma((NCH, 4)), dma((NCH, 4)),
            dma((NCH // 2,)), dma((NCH // 2,)),
        ],
        compiler_params=pltpu.CompilerParams(
            collective_id=0, has_side_effects=True, vmem_limit_bytes=60 * 1024 * 1024),
    )(h_values, h_scales, dy_values, dy_scales)


def solution(mesh):
    placed = P(("dp", "tensor"), None)
    return jax.shard_map(
        shards, mesh=mesh, in_specs=(placed,) * 4, out_specs=P("dp", "tensor"), check_vma=False)
```

time: 345 us -> 140 us (0.41)
  Pallas kernels: 0 us -> 136 us
  waiting for transfers between devices: 112 us -> 0 us
  blocking collectives: 80.1 us -> 0 us
  matrix products: 72.7 us -> 0 us
  local copies, waits for them, and re-layouts: 28.8 us -> 3.24 us
  other arithmetic: 21.1 us -> 0 us
  starting transfers between devices: 15.6 us -> 0 us
  between operations: 13.5 us -> 0.01 us
    pallas_call x0 -> x1, Pallas kernels: none -> 136 us  [shards(): pl.pallas_call(kernel, out_shape=jax.ShapeDtypeStruct((256, 1024), BF16),...]
    reduce_scatter x1 -> x0, waiting for transfers between devices: 107 us -> none  [shards(): lax.psum_scatter(group_product(grad_q, grad_scale, hidden_q, hidden_scale...]
    all_gather x1 -> x0, blocking collectives: 80.1 us -> none  [shards(): lax.all_gather(dy_scales, 'tensor', axis=0, tiled=True)]
    dot_general x6 -> x0, matrix products: 72.7 us -> none  [group_product(): lax.dot_general(grad_block, hidden_block, (((0,), (0,)), ((), ())), prefe...]
    mul x4 -> x0, local copies, waits for them, and re-layouts: 24.1 us -> none  [dequantize(): widened = widened * scales.astype(jnp.float32)[:, :, None]]
    all_to_all x2 -> x0, starting transfers between devices: 15.6 us -> none  [the longest x1 9.94 us: shards(): lax.all_to_all(h_scales, 'tensor', split_axis=1, concat_axis=0, tiled=True)]
    reduce_max x2 -> x0, other arithmetic: 11.1 us -> none  [requantize(): largest = jnp.max(jnp.abs(blocked), axis=1)]
    convert_element_type x7 -> x0, other arithmetic: 9.97 us -> none  [the longest x2 8.04 us: requantize(): (blocked / column_scale.astype(jnp.float32)[:, None, :]).astype(jnp.bfloa...]
  transfers between devices with their start and end apart: 4 -> 0, of which waited for: 2 -> 0; matrix products, arithmetic and copies ran while one was open for 10% -> 0% of each run, Pallas kernels for 0% -> 0%
where the time goes in v1:
time: 140 us; the launch traced here: 139 us
  Pallas kernels  136 us (97%)
  local copies, waits for them, and re-layouts  3.24 us (2%)
    pallas_call x1, Pallas kernels, shards(): pl.pallas_call(kernel, out_shape=jax.ShapeDtypeStruct((256, 1024), BF16),...  136 us
    unnamed x2, local copies, waits for them, and re-layouts  3.24 us

profile of v1, /device:TPU:2, one launch (start us, length us, event | category | flops | bytes accessed | tf_op | source)
XLA Modules:
  0.0 139.4 jit_solution(4889220994243877312)
XLA Ops:
  0.0 1.4 copy.5.ds
  1.4 136.1 %shard_map.46 = bf16[256,1024]{1,0:T(8,128)(2,1)} custom-call(bf16[48,16384]{1,0:T(8,128)(2,1)} %hv.1, bf16[48,128]{1,0:T(8,128)(2,1)} %hs.1, bf16[48,4096]{1,0:T(8,128)(2,1)} %dv.1, bf16[48,32]{1,0:T(8,128)(2,1)} %copy.5.ds), custom_call_target="tpu_custom_call" | custom-call | tf_op jit(solution)/shard_map/pallas_call | solution.py:255
  137.5 1.9 %copy.7 = bf16[256,1024]{1,0:T(8,128)(2,1)} copy(bf16[256,1024]{1,0:T(8,128)(2,1)} %shard_map.46) | data formatting | bytes 1048576

commit v2 on v0

v2 whole, which is shorter than its diff:
```python
import jax
import jax.numpy as jnp
from jax import lax
from jax.experimental import pallas as pl
from jax.experimental.pallas import tpu as pltpu
from jax.sharding import PartitionSpec as P

QBLOCK = 128
MESH = pl.DeviceIdType.MESH
XN, YN, ZN = 4, 4, 8
TOK = 48
LINE = ZN * TOK
KTOK = XN * LINE
HALF = 512
COLS = 2048
NCH = 8
W = COLS // NCH
F32, BF16 = jnp.float32, jnp.bfloat16
NT = (((1,), (1,)), ((), ()))
ORDER = (
    ("dy",), ("bar",), ("x0",), ("h", 0), ("h", 1), ("s", 0, 0), ("s", 1, 0), ("r", 0), ("r", 1), ("f", 0),
    ("s", 0, 1), ("h", 2), ("f", 1), ("s", 0, 2), ("h", 3), ("r", 2), ("s", 0, 3), ("s", 1, 1), ("f", 2), ("h", 4),
    ("r", 3), ("q", 0), ("P", 0, 0), ("P", 0, 1), ("P", 0, 2), ("s", 1, 2), ("f", 3), ("A", 0, 0), ("h", 5),
    ("A", 0, 1), ("A", 0, 2), ("B", 0, 0), ("P", 0, 3), ("r", 4), ("B", 0, 1), ("B", 0, 2), ("A", 0, 3),
    ("E", 0, 0), ("s", 1, 3), ("h", 6), ("E", 0, 1), ("E", 0, 2), ("B", 0, 3), ("h", 7), ("f", 4), ("r", 5),
    ("E", 0, 3), ("q", 1), ("P", 1, 0), ("P", 1, 1), ("P", 1, 2), ("P", 1, 3), ("P", 0, 4), ("f", 5), ("r", 6),
    ("A", 1, 0), ("A", 1, 1), ("P", 1, 4), ("A", 1, 2), ("A", 1, 3), ("A", 0, 4), ("A", 1, 4), ("B", 1, 0),
    ("r", 7), ("P", 0, 5), ("P", 1, 5), ("B", 1, 1), ("B", 1, 2), ("A", 0, 5), ("A", 1, 5), ("B", 1, 3), ("f", 6),
    ("B", 0, 4), ("B", 1, 4), ("E", 1, 0), ("E", 1, 1), ("f", 7), ("E", 1, 2), ("B", 0, 5), ("P", 0, 6),
    ("P", 1, 6), ("B", 1, 5), ("E", 1, 3), ("E", 0, 4), ("A", 0, 6), ("P", 0, 7), ("A", 1, 6), ("E", 1, 4),
    ("P", 1, 7), ("E", 0, 5), ("E", 1, 5), ("A", 0, 7), ("A", 1, 7), ("B", 0, 6), ("B", 1, 6), ("B", 0, 7),
    ("B", 1, 7), ("E", 0, 6), ("E", 1, 6), ("E", 0, 7), ("E", 1, 7), ("END",),
)


def requantize(block):
    largest = jnp.max(jnp.abs(block), axis=0, keepdims=True)
    scale = ((largest + 1e-6) / 448.0).astype(BF16).astype(F32)
    quantized = (block * (1.0 / scale)).astype(BF16).astype(F32)
    return (quantized * scale).astype(BF16)


def kernel(hv_hbm, hs_hbm, dv_hbm, ds_hbm, out,
           hv, hs, dv, ds, eye, dyp, gat, hsend, hz, hx, gt, px, pr, po,
           sp, sm, rp, rm, cp, cm, qp, qm, fb, fr,
           ld, hss, hrs, dxs, dxr, dzs, dzr, xss, xrs, xfs, xfr, cs, cr, ys, yr, fs, frs):
    dp, t = lax.axis_index("dp"), lax.axis_index("tensor")
    c, xh, y = dp % 2, (dp // 2) % 2, dp // 4
    xl, z = t // 8, t % 8
    x = xh * 2 + xl

    def dev(x_=None, y_=None, z_=None, c_=None):
        x_ = x if x_ is None else x_
        y_ = y if y_ is None else y_
        z_ = z if z_ is None else z_
        c_ = c if c_ is None else c_
        return ((y_ * 2 + x_ // 2) * 2 + c_, (x_ % 2) * 8 + z_)

    def send(src, dst, ssem, rsem, to):
        return pltpu.make_async_remote_copy(
            src_ref=src, dst_ref=dst, send_sem=ssem, recv_sem=rsem, device_id=to, device_id_type=MESH)

    def zrow(zs):
        return pl.ds(pl.multiple_of(zs * TOK, 16), TOK)

    def xrow(xs, lo=0, n=LINE):
        return pl.ds(pl.multiple_of(xs * LINE + lo, 16), n)

    barrier = pltpu.get_barrier_semaphore()
    peers = ([dev(x_=(x + d) % XN) for d in range(1, XN)] + [dev(y_=(y + d) % YN) for d in (1, 3)]
             + [dev(z_=(z + d) % ZN) for d in range(1, ZN)] + [dev(c_=1 - c)])
    for peer in peers:
        pl.semaphore_signal(barrier, inc=1, device_id=peer, device_id_type=MESH)

    loads = [pltpu.make_async_copy(a, b, ld.at[n])
             for n, (a, b) in enumerate(((hv_hbm, hv), (hs_hbm, hs), (dv_hbm, dv), (ds_hbm, ds)))]
    for cpy in loads:
        cpy.start()
    eye[...] = (lax.broadcasted_iota(jnp.int32, (256, 256), 0)
                == lax.broadcasted_iota(jnp.int32, (256, 256), 1)).astype(F32).astype(BF16)
    for cpy in loads:
        cpy.wait()

    zu, zd = dev(z_=(z + 1) % ZN), dev(z_=(z + 7) % ZN)
    xu, xd = dev(x_=(x + 1) % XN), dev(x_=(x + 3) % XN)
    yu, yd = dev(y_=(y + 1) % YN), dev(y_=(y + 3) % YN)
    partner, across = dev(c_=1 - c), dev(x_=xh * 2 + 1 - xl)
    xup, xdn = (x + 3) % XN, (x + 1) % XN
    y1, y2, y3 = (y + 1) % YN, (y + 2) % YN, (y + 3) % YN
    per = NCH // 2

    x_dy = [[send(dyp.at[h, (x + d) % XN], gat.at[h, x, zrow(z)], dxs.at[h, d - 1], dxr.at[h, d - 1],
                  dev(x_=(x + d) % XN)) for d in range(1, XN)] for h in range(2)]
    z_h = [[send(hsend.at[k, (z + d) % ZN], hz.at[k, zrow(z)], hss.at[k, n], hrs.at[k, n], dev(z_=(z + d) % ZN))
            for n, d in enumerate((1, 7, 2, 6, 3, 5, 4))] for k in range(NCH)]

    def ring(h, s):
        lo, hi = (slice(0, 2), slice(2, 4)) if s == 3 else (slice(None), slice(None))
        up, dn = gat.at[h, lo, zrow((z + 8 - s) % ZN)], gat.at[h, hi, zrow((z + s) % ZN)]
        return (send(up, up, dzs.at[h, 0, s], dzr.at[h, 0, s], zu), send(dn, dn, dzs.at[h, 1, s], dzr.at[h, 1, s], zd))

    z_dy = [[ring(h, s) for s in range(4)] for h in range(2)]

    def x_first(k):
        mine = hx.at[k, xrow(x)]
        return (send(mine, mine, xss.at[k, 0], xrs.at[k, 0], xu), send(mine, mine, xss.at[k, 1], xrs.at[k, 1], xd))

    def x_second(k):
        up, dn = hx.at[k, xrow(xup, 0, LINE // 2)], hx.at[k, xrow(xdn, LINE // 2, LINE // 2)]
        return (send(up, up, xfs.at[k, 0], xfr.at[k, 0], xu), send(dn, dn, xfs.at[k, 1], xfr.at[k, 1], xd))

    x_h = [x_first(k) for k in range(NCH)]
    x_f = [x_second(k) for k in range(NCH)]
    core = [send(px.at[k], pr.at[k], cs.at[k], cr.at[k], partner) for k in range(NCH)]
    y_a = [(send(sp.at[k], rp.at[k], ys.at[k, 0], yr.at[k, 0], yu),
            send(sm.at[k], rm.at[k], ys.at[k, 1], yr.at[k, 1], yd)) for k in range(NCH)]
    y_b = [(send(cp.at[k], qp.at[k], ys.at[k, 2], yr.at[k, 2], yu),
            send(cm.at[k], qm.at[k], ys.at[k, 3], yr.at[k, 3], yd)) for k in range(NCH)]

    def swap(j, k):
        return send(fb.at[k], fr.at[j], fs.at[j], frs.at[j], across)

    def start(group):
        for cpy in group:
            cpy.start()

    def arrive(group):
        for cpy in group:
            cpy.wait_recv()

    def dequantize_dy():
        for j in range(32):
            y_, a_, c_, b_ = j // 8, (j // 4) % 2, (j // 2) % 2, j % 2
            val = dv[:, j * 128:(j + 1) * 128].astype(F32) * scales[:, j:j + 1]
            dyp[c_, a_ * 2 + b_, :, y_ * 128:(y_ + 1) * 128] = val.astype(BF16)
        for h in range(2):
            gat[h, x, zrow(z), :] = dyp[h, x]

    def send_dy():
        for h in range(2):
            start(x_dy[h])

    def send_h(k):
        for zz in range(ZN):
            for i in range(W // 128):
                col = k * W + i * 128
                j = ((col // 1024) * 8 + zz) * 8 + (col % 1024) // 128
                val = hv[:, j * 128:(j + 1) * 128].astype(F32) * hs[:, j:j + 1].astype(F32)
                hsend[k, zz, :, i * 128:(i + 1) * 128] = val.astype(BF16)
        start(z_h[k])
        hz[k, zrow(z), :] = hsend[k, z]

    def ring_dy(h, s):
        arrive(z_dy[h][s - 1] if s else x_dy[h])
        start(z_dy[h][s])

    def requantize_h(k):
        arrive(z_h[k])

        @pl.loop(0, W // 128)
        def _(i):
            lanes = pl.ds(pl.multiple_of(i * 128, 128), 128)
            for b in range(LINE // QBLOCK):
                hx[k, xrow(x, b * QBLOCK, QBLOCK), lanes] = requantize(
                    hz[k, b * QBLOCK:(b + 1) * QBLOCK, lanes].astype(F32))

        start(x_h[k])

    def forward_h(k):
        arrive(x_h[k])
        start(x_f[k])

    def requantize_dy(h):
        arrive(z_dy[h][3])
        for b in range(KTOK // 256):

            @pl.loop(0, HALF // 256)
            def _(i):
                at = pl.ds(pl.multiple_of(i * 256, 256), 256)
                vals = [requantize(gat[h, n // 3, (n % 3) * QBLOCK:(n % 3 + 1) * QBLOCK, at].astype(F32))
                        for n in (2 * b, 2 * b + 1)]
                turned = lax.dot_general(eye[...], jnp.concatenate(vals, 0), NT, preferred_element_type=F32)
                gt[pl.ds(pl.multiple_of(h * HALF + i * 256, 256), 256), b * 256:(b + 1) * 256] = turned.astype(BF16)

    def product(h, k):
        arrived = [x_f[k]]
        for group in arrived:
            if h == first_half[k]:
                arrive(group)

        @pl.when(c != h)
        def _():
            px[k] = jnp.dot(gt[h * HALF:(h + 1) * HALF, :], hx[k], preferred_element_type=F32).astype(BF16)
            core[k].start()

        @pl.when(c == h)
        def _():
            po[k] = jnp.dot(gt[h * HALF:(h + 1) * HALF, :], hx[k], preferred_element_type=F32)

    def part(k, yy, lo):
        return po[k, pl.ds(pl.multiple_of(yy * 128 + lo, 64), 64), :]

    def reduce_first(h, k):
        @pl.when(c == h)
        def _():
            core[k].wait_recv()
            po[k] = po[k] + pr[k].astype(F32)
            sp[k, 0] = part(k, y2, 0).astype(BF16)
            sp[k, 1] = part(k, y1, 64).astype(BF16)
            sm[k, 0] = part(k, y2, 64).astype(BF16)
            sm[k, 1] = part(k, y3, 0).astype(BF16)
            start(y_a[k])

    def reduce_second(h, k):
        @pl.when(c == h)
        def _():
            arrive(y_a[k])
            cp[k] = (part(k, y1, 0) + rp[k, 0].astype(F32)).astype(BF16)
            cm[k] = (part(k, y3, 64) + rm[k, 0].astype(F32)).astype(BF16)
            start(y_b[k])

    def finish(h, k):
        @pl.when(c == h)
        def _():
            arrive(y_b[k])
            fb[k, 0:64] = (part(k, y, 0) + qp[k].astype(F32) + rm[k, 1].astype(F32)).astype(BF16)
            fb[k, 64:128] = (part(k, y, 64) + qm[k].astype(F32) + rp[k, 1].astype(F32)).astype(BF16)

            @pl.when(xl != k // per)
            def _():
                swap(k % per, k).start()

    def conclude():
        mine_rows = pl.ds(pl.multiple_of(xl * 128, 128), 128)
        other_rows = pl.ds(pl.multiple_of((1 - xl) * 128, 128), 128)
        for j in range(per):
            out[mine_rows, j * W:(j + 1) * W] = fb[xl * per + j]
        for j in range(per):
            swap(j, (1 - xl) * per + j).wait()
            out[other_rows, j * W:(j + 1) * W] = fr[j]
        for group in x_dy + z_h + z_dy[0] + z_dy[1] + x_h + x_f + [core] + y_a + y_b:
            for cpy in group:
                cpy.wait_send()

    scales = lax.dot_general(eye[0:TOK, 0:TOK], ds[...], NT, preferred_element_type=F32)
    first_half = {}
    for step in ORDER:
        if step[0] == "P":
            first_half.setdefault(step[2], step[1])
    steps = dict(dy=dequantize_dy, bar=lambda: pl.semaphore_wait(barrier, len(peers)), x0=send_dy, h=send_h,
                 s=ring_dy, r=requantize_h, f=forward_h, q=requantize_dy, P=product, A=reduce_first,
                 B=reduce_second, E=finish, END=conclude)
    for step in ORDER:
        steps[step[0]](*step[1:])


def shards(h_values, h_scales, dy_values, dy_scales):
    dma = pltpu.SemaphoreType.DMA
    anywhere = pl.BlockSpec(memory_space=pl.ANY)
    return pl.pallas_call(
        kernel,
        out_shape=jax.ShapeDtypeStruct((256, 1024), BF16),
        in_specs=[anywhere] * 4,
        out_specs=pl.BlockSpec(memory_space=pltpu.VMEM),
        scratch_shapes=[
            pltpu.VMEM((TOK, 16384), BF16),
            pltpu.VMEM((TOK, 128), BF16),
            pltpu.VMEM((TOK, 4096), BF16),
            pltpu.VMEM((32, TOK), BF16),
            pltpu.VMEM((256, 256), BF16),
            pltpu.VMEM((2, XN, TOK, HALF), BF16),
            pltpu.VMEM((2, XN, LINE, HALF), BF16),
            pltpu.VMEM((NCH, ZN, TOK, W), BF16),
            pltpu.VMEM((NCH, LINE, W), BF16),
            pltpu.VMEM((NCH, KTOK, W), BF16),
            pltpu.VMEM((2 * HALF, KTOK), BF16),
            pltpu.VMEM((NCH, HALF, W), BF16),
            pltpu.VMEM((NCH, HALF, W), BF16),
            pltpu.VMEM((NCH, HALF, W), F32),
            pltpu.VMEM((NCH, 2, 64, W), BF16),
            pltpu.VMEM((NCH, 2, 64, W), BF16),
            pltpu.VMEM((NCH, 2, 64, W), BF16),
            pltpu.VMEM((NCH, 2, 64, W), BF16),
            pltpu.VMEM((NCH, 64, W), BF16),
            pltpu.VMEM((NCH, 64, W), BF16),
            pltpu.VMEM((NCH, 64, W), BF16),
            pltpu.VMEM((NCH, 64, W), BF16),
            pltpu.VMEM((NCH, 128, W), BF16),
            pltpu.VMEM((NCH // 2, 128, W), BF16),
            dma((4,)),
            dma((NCH, 7)), dma((NCH, 7)),
            dma((2, 3)), dma((2, 3)),
            dma((2, 2, 4)), dma((2, 2, 4)),
            dma((NCH, 2)), dma((NCH, 2)),
            dma((NCH, 2)), dma((NCH, 2)),
            dma((NCH,)), dma((NCH,)),
            dma((NCH, 4)), dma((NCH, 4)),
            dma((NCH // 2,)), dma((NCH // 2,)),
        ],
        compiler_params=pltpu.CompilerParams(
            collective_id=0, has_side_effects=True, vmem_limit_bytes=60 * 1024 * 1024),
    )(h_values, h_scales, dy_values, dy_scales.T)


def solution(mesh):
    placed = P(("dp", "tensor"), None)
    return jax.shard_map(
        shards, mesh=mesh, in_specs=(placed,) * 4, out_specs=P("dp", "tensor"), check_vma=False)
```

time: 345 us -> 107 us (0.31)
  waiting for transfers between devices: 112 us -> 0 us
  Pallas kernels: 0 us -> 105 us
  blocking collectives: 80.1 us -> 0 us
  matrix products: 72.7 us -> 0 us
  local copies, waits for them, and re-layouts: 28.8 us -> 1.87 us
  other arithmetic: 21.1 us -> 0 us
  starting transfers between devices: 15.6 us -> 0 us
  between operations: 13.5 us -> 0.01 us
    reduce_scatter x1 -> x0, waiting for transfers between devices: 107 us -> none  [shards(): lax.psum_scatter(group_product(grad_q, grad_scale, hidden_q, hidden_scale...]
    pallas_call x0 -> x1, Pallas kernels: none -> 105 us  [shards(): pl.pallas_call(kernel, out_shape=jax.ShapeDtypeStruct((256, 1024), BF16),...]
    all_gather x1 -> x0, blocking collectives: 80.1 us -> none  [shards(): lax.all_gather(dy_scales, 'tensor', axis=0, tiled=True)]
    dot_general x6 -> x0, matrix products: 72.7 us -> none  [group_product(): lax.dot_general(grad_block, hidden_block, (((0,), (0,)), ((), ())), prefe...]
    mul x4 -> x0, local copies, waits for them, and re-layouts: 24.1 us -> none  [dequantize(): widened = widened * scales.astype(jnp.float32)[:, :, None]]
    all_to_all x2 -> x0, starting transfers between devices: 15.6 us -> none  [the longest x1 9.94 us: shards(): lax.all_to_all(h_scales, 'tensor', split_axis=1, concat_axis=0, tiled=True)]
    reduce_max x2 -> x0, other arithmetic: 11.1 us -> none  [requantize(): largest = jnp.max(jnp.abs(blocked), axis=1)]
    convert_element_type x7 -> x0, other arithmetic: 9.97 us -> none  [the longest x2 8.04 us: requantize(): (blocked / column_scale.astype(jnp.float32)[:, None, :]).astype(jnp.bfloa...]
  transfers between devices with their start and end apart: 4 -> 0, of which waited for: 2 -> 0; matrix products, arithmetic and copies ran while one was open for 10% -> 0% of each run, Pallas kernels for 0% -> 0%
where the time goes in v2:
time: 107 us
  Pallas kernels  105 us (98%)
  local copies, waits for them, and re-layouts  1.87 us (2%)
    pallas_call x1, Pallas kernels, shards(): pl.pallas_call(kernel, out_shape=jax.ShapeDtypeStruct((256, 1024), BF16),...  105 us

profile of v2, /device:TPU:2, one launch (start us, length us, event | category | flops | bytes accessed | tf_op | source)
XLA Modules:
  0.0 107.2 jit_solution(10157837294727369002)
XLA Ops:
  0.0 105.3 %shard_map.46 = bf16[256,1024]{1,0:T(8,128)(2,1)} custom-call(bf16[48,16384]{1,0:T(8,128)(2,1)} %hv_hbm.1, bf16[48,128]{1,0:T(8,128)(2,1)} %hs_hbm.1, bf16[48,4096]{1,0:T(8,128)(2,1)} %dv_hbm.1, bf16[32,48]{1,0:T(8,128)(2,1)} %bitcast.1), custom_call_target="tpu_custom_call" | custom-call | tf_op jit(solution)/shard_map/pallas_call | solution.py:260
  105.3 1.9 %copy.6 = bf16[256,1024]{1,0:T(8,128)(2,1)} copy(bf16[256,1024]{1,0:T(8,128)(2,1)} %shard_map.46) | data formatting | bytes 1048576

commit v3 on v2

v3 whole, which is shorter than its diff:
```python
import jax
import jax.numpy as jnp
from jax import lax
from jax.experimental import pallas as pl
from jax.experimental.pallas import tpu as pltpu
from jax.sharding import PartitionSpec as P

QBLOCK = 128
MESH = pl.DeviceIdType.MESH
XN, YN, ZN = 4, 4, 8
TOK = 48
LINE = ZN * TOK
KTOK = XN * LINE
HALF = 512
COLS = 2048
WIDTHS = (128, 384, 512, 512, 256, 128, 128)
NCH = len(WIDTHS)
STARTS = tuple(sum(WIDTHS[:k]) for k in range(NCH))
OWNER = tuple(start // 1024 for start in STARTS)
F32, BF16 = jnp.float32, jnp.bfloat16
NT = (((1,), (1,)), ((), ()))
ORDER = (
    ("dy",), ("bar",), ("h", 1), ("x0",), ("h", 2), ("s", 0, 0), ("r", 1), ("h", 3), ("r", 2), ("f", 1),
    ("s", 0, 1), ("f", 2), ("s", 1, 0), ("s", 0, 2), ("r", 3), ("h", 0), ("s", 0, 3), ("s", 1, 1), ("r", 0),
    ("f", 3), ("h", 4), ("q", 0), ("s", 1, 2), ("f", 0), ("P", 0, 1), ("P", 0, 2), ("h", 5), ("P", 0, 3), ("r", 4),
    ("A", 0, 2), ("A", 0, 1), ("A", 0, 3), ("P", 0, 0), ("s", 1, 3), ("h", 6), ("A", 0, 0), ("B", 0, 2), ("r", 5),
    ("B", 0, 1), ("B", 0, 3), ("f", 4), ("q", 1), ("r", 6), ("f", 5), ("P", 1, 3), ("P", 1, 2), ("P", 0, 4),
    ("A", 1, 3), ("P", 1, 1), ("A", 1, 2), ("f", 6), ("P", 1, 4), ("A", 0, 4), ("P", 0, 5), ("B", 0, 0),
    ("A", 1, 1), ("P", 1, 0), ("A", 1, 4), ("P", 1, 5), ("B", 1, 3), ("P", 1, 6), ("A", 0, 5), ("B", 1, 2),
    ("P", 0, 6), ("A", 1, 5), ("B", 0, 4), ("A", 1, 6), ("A", 1, 0), ("E", 0, 3), ("A", 0, 6), ("E", 0, 2),
    ("B", 1, 4), ("B", 1, 1), ("E", 1, 3), ("E", 1, 2), ("E", 0, 1), ("B", 1, 5), ("B", 0, 5), ("B", 1, 0),
    ("B", 1, 6), ("B", 0, 6), ("E", 1, 4), ("E", 0, 4), ("E", 1, 1), ("E", 0, 0), ("E", 1, 5), ("E", 0, 5),
    ("E", 1, 0), ("E", 1, 6), ("E", 0, 6), ("END",),
)


def requantize(block):
    largest = jnp.max(jnp.abs(block), axis=0, keepdims=True)
    scale = ((largest + 1e-6) / 448.0).astype(BF16).astype(F32)
    quantized = (block * (1.0 / scale)).astype(BF16).astype(F32)
    return (quantized * scale).astype(BF16)


def kernel(hv_hbm, hs_hbm, dv_hbm, ds_hbm, out,
           hv, hs, dv, ds, eye, dyp, gat, hsend, hz, hx, gt, px, pr, po,
           sp, sm, rp, rm, cp, cm, qp, qm, fb, fr,
           ld, hss, hrs, dxs, dxr, dzs, dzr, xss, xrs, xfs, xfr, cs, cr, ys, yr, fs, frs):
    dp, t = lax.axis_index("dp"), lax.axis_index("tensor")
    c, xh, y = dp % 2, (dp // 2) % 2, dp // 4
    xl, z = t // 8, t % 8
    x = xh * 2 + xl

    def dev(x_=None, y_=None, z_=None, c_=None):
        x_ = x if x_ is None else x_
        y_ = y if y_ is None else y_
        z_ = z if z_ is None else z_
        c_ = c if c_ is None else c_
        return ((y_ * 2 + x_ // 2) * 2 + c_, (x_ % 2) * 8 + z_)

    def send(src, dst, ssem, rsem, to):
        return pltpu.make_async_remote_copy(
            src_ref=src, dst_ref=dst, send_sem=ssem, recv_sem=rsem, device_id=to, device_id_type=MESH)

    def zrow(zs):
        return pl.ds(pl.multiple_of(zs * TOK, 16), TOK)

    def xrow(xs, lo=0, n=LINE):
        return pl.ds(pl.multiple_of(xs * LINE + lo, 16), n)

    barrier = pltpu.get_barrier_semaphore()
    peers = ([dev(x_=(x + d) % XN) for d in range(1, XN)] + [dev(y_=(y + d) % YN) for d in (1, 3)]
             + [dev(z_=(z + d) % ZN) for d in range(1, ZN)] + [dev(c_=1 - c)])
    for peer in peers:
        pl.semaphore_signal(barrier, inc=1, device_id=peer, device_id_type=MESH)

    loads = [pltpu.make_async_copy(a, b, ld.at[n])
             for n, (a, b) in enumerate(((hv_hbm, hv), (hs_hbm, hs), (dv_hbm, dv), (ds_hbm, ds)))]
    for cpy in loads:
        cpy.start()
    eye[...] = (lax.broadcasted_iota(jnp.int32, (256, 256), 0)
                == lax.broadcasted_iota(jnp.int32, (256, 256), 1)).astype(F32).astype(BF16)
    for cpy in loads:
        cpy.wait()

    zu, zd = dev(z_=(z + 1) % ZN), dev(z_=(z + 7) % ZN)
    xu, xd = dev(x_=(x + 1) % XN), dev(x_=(x + 3) % XN)
    yu, yd = dev(y_=(y + 1) % YN), dev(y_=(y + 3) % YN)
    partner, across = dev(c_=1 - c), dev(x_=xh * 2 + 1 - xl)
    xup, xdn = (x + 3) % XN, (x + 1) % XN
    y1, y2, y3 = (y + 1) % YN, (y + 2) % YN, (y + 3) % YN

    x_dy = [[send(dyp.at[h, (x + d) % XN], gat.at[h, x, zrow(z)], dxs.at[h, d - 1], dxr.at[h, d - 1],
                  dev(x_=(x + d) % XN)) for d in range(1, XN)] for h in range(2)]
    z_h = [[send(hsend[k].at[(z + d) % ZN], hz[k].at[zrow(z)], hss.at[k, n], hrs.at[k, n], dev(z_=(z + d) % ZN))
            for n, d in enumerate((1, 7, 2, 6, 3, 5, 4))] for k in range(NCH)]

    def ring(h, s):
        lo, hi = (slice(0, 2), slice(2, 4)) if s == 3 else (slice(None), slice(None))
        up, dn = gat.at[h, lo, zrow((z + 8 - s) % ZN)], gat.at[h, hi, zrow((z + s) % ZN)]
        return (send(up, up, dzs.at[h, 0, s], dzr.at[h, 0, s], zu), send(dn, dn, dzs.at[h, 1, s], dzr.at[h, 1, s], zd))

    z_dy = [[ring(h, s) for s in range(4)] for h in range(2)]

    def x_first(k):
        mine = hx[k].at[xrow(x)]
        return (send(mine, mine, xss.at[k, 0], xrs.at[k, 0], xu), send(mine, mine, xss.at[k, 1], xrs.at[k, 1], xd))

    def x_second(k):
        up, dn = hx[k].at[xrow(xup, 0, LINE // 2)], hx[k].at[xrow(xdn, LINE // 2, LINE // 2)]
        return (send(up, up, xfs.at[k, 0], xfr.at[k, 0], xu), send(dn, dn, xfs.at[k, 1], xfr.at[k, 1], xd))

    x_h = [x_first(k) for k in range(NCH)]
    x_f = [x_second(k) for k in range(NCH)]
    core = [send(px[k], pr[k], cs.at[k], cr.at[k], partner) for k in range(NCH)]
    y_a = [(send(sp[k], rp[k], ys.at[k, 0], yr.at[k, 0], yu),
            send(sm[k], rm[k], ys.at[k, 1], yr.at[k, 1], yd)) for k in range(NCH)]
    y_b = [(send(cp[k], qp[k], ys.at[k, 2], yr.at[k, 2], yu),
            send(cm[k], qm[k], ys.at[k, 3], yr.at[k, 3], yd)) for k in range(NCH)]

    swap = [send(fb[k], fr[k], fs.at[k], frs.at[k], across) for k in range(NCH)]

    def start(group):
        for cpy in group:
            cpy.start()

    def arrive(group):
        for cpy in group:
            cpy.wait_recv()

    def dequantize_dy():
        for j in range(32):
            y_, a_, c_, b_ = j // 8, (j // 4) % 2, (j // 2) % 2, j % 2
            val = dv[:, j * 128:(j + 1) * 128].astype(F32) * scales[:, j:j + 1]
            dyp[c_, a_ * 2 + b_, :, y_ * 128:(y_ + 1) * 128] = val.astype(BF16)
        for h in range(2):
            gat[h, x, zrow(z), :] = dyp[h, x]

    def send_dy():
        for h in range(2):
            start(x_dy[h])

    def dequantize_h(k):
        for zz in range(ZN):
            for i in range(WIDTHS[k] // 128):
                col = STARTS[k] + i * 128
                j = ((col // 1024) * 8 + zz) * 8 + (col % 1024) // 128
                val = hv[:, j * 128:(j + 1) * 128].astype(F32) * hs[:, j:j + 1].astype(F32)
                hsend[k][zz, :, i * 128:(i + 1) * 128] = val.astype(BF16)

    def send_h(k):
        if k:
            dequantize_h(k)
        start(z_h[k])
        hz[k][zrow(z), :] = hsend[k][z]

    def ring_dy(h, s):
        arrive(z_dy[h][s - 1] if s else x_dy[h])
        start(z_dy[h][s])

    def requantize_h(k):
        arrive(z_h[k])

        @pl.loop(0, WIDTHS[k] // 128)
        def _(i):
            lanes = pl.ds(pl.multiple_of(i * 128, 128), 128)
            for b in range(LINE // QBLOCK):
                hx[k][xrow(x, b * QBLOCK, QBLOCK), lanes] = requantize(
                    hz[k][b * QBLOCK:(b + 1) * QBLOCK, lanes].astype(F32))

        start(x_h[k])

    def forward_h(k):
        arrive(x_h[k])
        start(x_f[k])

    def requantize_dy(h):
        arrive(z_dy[h][3])
        for b in range(KTOK // 256):

            @pl.loop(0, HALF // 256)
            def _(i):
                at = pl.ds(pl.multiple_of(i * 256, 256), 256)
                vals = [requantize(gat[h, n // 3, (n % 3) * QBLOCK:(n % 3 + 1) * QBLOCK, at].astype(F32))
                        for n in (2 * b, 2 * b + 1)]
                turned = lax.dot_general(eye[...], jnp.concatenate(vals, 0), NT, preferred_element_type=F32)
                gt[pl.ds(pl.multiple_of(h * HALF + i * 256, 256), 256), b * 256:(b + 1) * 256] = turned.astype(BF16)

    def product(h, k):
        if h == first_half[k]:
            arrive(x_f[k])

        @pl.when(c != h)
        def _():
            px[k][...] = jnp.dot(gt[h * HALF:(h + 1) * HALF, :], hx[k][...], preferred_element_type=F32).astype(BF16)
            core[k].start()

        @pl.when(c == h)
        def _():
            po[k][...] = jnp.dot(gt[h * HALF:(h + 1) * HALF, :], hx[k][...], preferred_element_type=F32)

    def part(k, yy, lo):
        return po[k][pl.ds(pl.multiple_of(yy * 128 + lo, 64), 64), :]

    def reduce_first(h, k):
        @pl.when(c == h)
        def _():
            core[k].wait_recv()
            po[k][...] = po[k][...] + pr[k][...].astype(F32)
            sp[k][0] = part(k, y2, 0).astype(BF16)
            sp[k][1] = part(k, y1, 64).astype(BF16)
            sm[k][0] = part(k, y2, 64).astype(BF16)
            sm[k][1] = part(k, y3, 0).astype(BF16)
            start(y_a[k])

    def reduce_second(h, k):
        @pl.when(c == h)
        def _():
            arrive(y_a[k])
            cp[k][...] = (part(k, y1, 0) + rp[k][0].astype(F32)).astype(BF16)
            cm[k][...] = (part(k, y3, 64) + rm[k][0].astype(F32)).astype(BF16)
            start(y_b[k])

    def finish(h, k):
        @pl.when(c == h)
        def _():
            arrive(y_b[k])
            low = (part(k, y, 0) + qp[k][...].astype(F32) + rm[k][1].astype(F32)).astype(BF16)
            high = (part(k, y, 64) + qm[k][...].astype(F32) + rp[k][1].astype(F32)).astype(BF16)

            @pl.when(xl == OWNER[k])
            def _():
                out[pl.ds(pl.multiple_of(xl * 128, 64), 64), columns(k)] = low
                out[pl.ds(pl.multiple_of(xl * 128 + 64, 64), 64), columns(k)] = high

            @pl.when(xl != OWNER[k])
            def _():
                fb[k][0:64] = low
                fb[k][64:128] = high
                swap[k].start()

    def columns(k):
        return slice(STARTS[k] % 1024, STARTS[k] % 1024 + WIDTHS[k])

    def conclude():
        for k in last_chunks:
            @pl.when(xl == OWNER[k])
            def _():
                swap[k].wait_recv()
                out[pl.ds(pl.multiple_of((1 - xl) * 128, 128), 128), columns(k)] = fr[k][...]

            @pl.when(xl != OWNER[k])
            def _():
                swap[k].wait_send()
        for group in x_dy + z_h + z_dy[0] + z_dy[1] + x_h + x_f:
            for cpy in group:
                cpy.wait_send()
        for k in range(NCH):
            for cpy in (core[k],) + y_a[k] + y_b[k]:
                cpy.wait_send()

    scales = lax.dot_general(eye[0:TOK, 0:TOK], ds[...], NT, preferred_element_type=F32)
    first_half, last_chunks = {}, []
    for step in ORDER:
        if step[0] == "P":
            first_half.setdefault(step[2], step[1])
        if step[0] == "E":
            last_chunks = [k for k in last_chunks if k != step[2]] + [step[2]]
    steps = dict(dy=dequantize_dy, bar=lambda: pl.semaphore_wait(barrier, len(peers)), x0=send_dy, h=send_h,
                 s=ring_dy, r=requantize_h, f=forward_h, q=requantize_dy, P=product, A=reduce_first,
                 B=reduce_second, E=finish, END=conclude)
    dequantize_h(0)
    for step in ORDER:
        steps[step[0]](*step[1:])


def shards(h_values, h_scales, dy_values, dy_scales):
    dma = pltpu.SemaphoreType.DMA
    anywhere = pl.BlockSpec(memory_space=pl.ANY)

    def chunks(shape, dtype=BF16):
        return [pltpu.VMEM(shape + (width,), dtype) for width in WIDTHS]

    return pl.pallas_call(
        kernel,
        out_shape=jax.ShapeDtypeStruct((256, 1024), BF16),
        in_specs=[anywhere] * 4,
        out_specs=pl.BlockSpec(memory_space=pltpu.VMEM),
        scratch_shapes=[
            pltpu.VMEM((TOK, 16384), BF16),
            pltpu.VMEM((TOK, 128), BF16),
            pltpu.VMEM((TOK, 4096), BF16),
            pltpu.VMEM((32, TOK), BF16),
            pltpu.VMEM((256, 256), BF16),
            pltpu.VMEM((2, XN, TOK, HALF), BF16),
            pltpu.VMEM((2, XN, LINE, HALF), BF16),
            chunks((ZN, TOK)),
            chunks((LINE,)),
            chunks((KTOK,)),
            pltpu.VMEM((2 * HALF, KTOK), BF16),
            chunks((HALF,)),
            chunks((HALF,)),
            chunks((HALF,), F32),
            chunks((2, 64)), chunks((2, 64)), chunks((2, 64)), chunks((2, 64)),
            chunks((64,)), chunks((64,)), chunks((64,)), chunks((64,)),
            chunks((128,)), chunks((128,)),
            dma((4,)),
            dma((NCH, 7)), dma((NCH, 7)),
            dma((2, 3)), dma((2, 3)),
            dma((2, 2, 4)), dma((2, 2, 4)),
            dma((NCH, 2)), dma((NCH, 2)),
            dma((NCH, 2)), dma((NCH, 2)),
            dma((NCH,)), dma((NCH,)),
            dma((NCH, 4)), dma((NCH, 4)),
            dma((NCH,)), dma((NCH,)),
        ],
        compiler_params=pltpu.CompilerParams(
            collective_id=0, has_side_effects=True, vmem_limit_bytes=60 * 1024 * 1024),
    )(h_values, h_scales, dy_values, dy_scales.T)


def solution(mesh):
    placed = P(("dp", "tensor"), None)
    return jax.shard_map(
        shards, mesh=mesh, in_specs=(placed,) * 4, out_specs=P("dp", "tensor"), check_vma=False)
```

time: 107 us -> 103 us (0.963)
  Pallas kernels: 105 us -> 101 us
    pallas_call x1, Pallas kernels: 105 us -> 101 us  [shards(): pl.pallas_call(kernel, out_shape=jax.ShapeDtypeStruct((256, 1024), BF16),...]
where the time goes in v3:
time: 103 us
  Pallas kernels  101 us (98%)
  local copies, waits for them, and re-layouts  1.87 us (2%)
    pallas_call x1, Pallas kernels, shards(): pl.pallas_call(kernel, out_shape=jax.ShapeDtypeStruct((256, 1024), BF16),...  101 us

profile of v3, /device:TPU:2, one launch (start us, length us, event | category | flops | bytes accessed | tf_op | source)
XLA Modules:
  0.0 102.8 jit_solution(4892461345793101319)
XLA Ops:
  0.0 100.9 %shard_map.46 = bf16[256,1024]{1,0:T(8,128)(2,1)} custom-call(bf16[48,16384]{1,0:T(8,128)(2,1)} %hv_hbm.1, bf16[48,128]{1,0:T(8,128)(2,1)} %hs_hbm.1, bf16[48,4096]{1,0:T(8,128)(2,1)} %dv_hbm.1, bf16[32,48]{1,0:T(8,128)(2,1)} %bitcast.1), custom_call_target="tpu_custom_call" | custom-call | tf_op jit(solution)/shard_map/pallas_call | solution.py:283
  101.0 1.9 %copy.6 = bf16[256,1024]{1,0:T(8,128)(2,1)} copy(bf16[256,1024]{1,0:T(8,128)(2,1)} %shard_map.46) | data formatting | bytes 1048576

commit v4 on v3

--- a/solution.py
+++ b/solution.py
@@ -20,17 +20,17 @@
 F32, BF16 = jnp.float32, jnp.bfloat16
 NT = (((1,), (1,)), ((), ()))
 ORDER = (
-    ("dy",), ("bar",), ("h", 1), ("x0",), ("h", 2), ("s", 0, 0), ("r", 1), ("h", 3), ("r", 2), ("f", 1),
-    ("s", 0, 1), ("f", 2), ("s", 1, 0), ("s", 0, 2), ("r", 3), ("h", 0), ("s", 0, 3), ("s", 1, 1), ("r", 0),
-    ("f", 3), ("h", 4), ("q", 0), ("s", 1, 2), ("f", 0), ("P", 0, 1), ("P", 0, 2), ("h", 5), ("P", 0, 3), ("r", 4),
-    ("A", 0, 2), ("A", 0, 1), ("A", 0, 3), ("P", 0, 0), ("s", 1, 3), ("h", 6), ("A", 0, 0), ("B", 0, 2), ("r", 5),
-    ("B", 0, 1), ("B", 0, 3), ("f", 4), ("q", 1), ("r", 6), ("f", 5), ("P", 1, 3), ("P", 1, 2), ("P", 0, 4),
-    ("A", 1, 3), ("P", 1, 1), ("A", 1, 2), ("f", 6), ("P", 1, 4), ("A", 0, 4), ("P", 0, 5), ("B", 0, 0),
-    ("A", 1, 1), ("P", 1, 0), ("A", 1, 4), ("P", 1, 5), ("B", 1, 3), ("P", 1, 6), ("A", 0, 5), ("B", 1, 2),
-    ("P", 0, 6), ("A", 1, 5), ("B", 0, 4), ("A", 1, 6), ("A", 1, 0), ("E", 0, 3), ("A", 0, 6), ("E", 0, 2),
-    ("B", 1, 4), ("B", 1, 1), ("E", 1, 3), ("E", 1, 2), ("E", 0, 1), ("B", 1, 5), ("B", 0, 5), ("B", 1, 0),
-    ("B", 1, 6), ("B", 0, 6), ("E", 1, 4), ("E", 0, 4), ("E", 1, 1), ("E", 0, 0), ("E", 1, 5), ("E", 0, 5),
-    ("E", 1, 0), ("E", 1, 6), ("E", 0, 6), ("END",),
+    ("dy",), ("bar",), ("h", 0), ("x0",), ("h", 3), ("r", 0), ("s", 0, 0), ("h", 1), ("r", 3), ("h", 2),
+    ("s", 0, 1), ("f", 0), ("f", 3), ("r", 1), ("s", 1, 0), ("s", 0, 2), ("r", 2), ("s", 1, 1), ("f", 1),
+    ("s", 0, 3), ("s", 1, 2), ("f", 2), ("h", 4), ("q", 0), ("P", 0, 1), ("P", 0, 3), ("P", 0, 0), ("s", 1, 3),
+    ("P", 0, 2), ("A", 0, 1), ("A", 0, 0), ("h", 6), ("h", 5), ("r", 4), ("A", 0, 3), ("A", 0, 2), ("q", 1),
+    ("B", 0, 3), ("r", 6), ("P", 1, 1), ("P", 1, 0), ("B", 0, 2), ("f", 4), ("B", 0, 1), ("P", 1, 3), ("A", 1, 1),
+    ("r", 5), ("P", 1, 2), ("A", 1, 3), ("f", 6), ("P", 0, 4), ("B", 1, 1), ("E", 0, 3), ("A", 1, 2), ("f", 5),
+    ("P", 1, 4), ("B", 1, 3), ("A", 0, 4), ("A", 1, 0), ("P", 1, 6), ("P", 0, 6), ("A", 1, 4), ("B", 1, 2),
+    ("P", 0, 5), ("P", 1, 5), ("E", 1, 1), ("A", 1, 6), ("A", 0, 6), ("E", 0, 2), ("A", 0, 5), ("A", 1, 5),
+    ("B", 1, 4), ("E", 1, 3), ("E", 0, 1), ("B", 0, 4), ("B", 1, 6), ("B", 1, 0), ("B", 0, 0), ("B", 0, 6),
+    ("B", 0, 5), ("E", 1, 2), ("B", 1, 5), ("E", 1, 4), ("E", 0, 4), ("E", 1, 6), ("E", 1, 0), ("E", 0, 0),
+    ("E", 0, 6), ("E", 0, 5), ("E", 1, 5), ("END",),
 )
 
 
@@ -44,7 +44,7 @@
 def kernel(hv_hbm, hs_hbm, dv_hbm, ds_hbm, out,
            hv, hs, dv, ds, eye, dyp, gat, hsend, hz, hx, gt, px, pr, po,
            sp, sm, rp, rm, cp, cm, qp, qm, fb, fr,
-           ld, hss, hrs, dxs, dxr, dzs, dzr, xss, xrs, xfs, xfr, cs, cr, ys, yr, fs, frs):
+           ld, hss, hrs, dxs, dxr, dzs, dzr, xss, xrs, xfs, xfr, cs, cr, ys, yr, fs, frs, os):
     dp, t = lax.axis_index("dp"), lax.axis_index("tensor")
     c, xh, y = dp % 2, (dp // 2) % 2, dp // 4
     xl, z = t // 8, t % 8
@@ -227,36 +227,43 @@
             low = (part(k, y, 0) + qp[k][...].astype(F32) + rm[k][1].astype(F32)).astype(BF16)
             high = (part(k, y, 64) + qm[k][...].astype(F32) + rp[k][1].astype(F32)).astype(BF16)
 
+            fb[k][0:64] = low
+            fb[k][64:128] = high
+
             @pl.when(xl == OWNER[k])
             def _():
-                out[pl.ds(pl.multiple_of(xl * 128, 64), 64), columns(k)] = low
-                out[pl.ds(pl.multiple_of(xl * 128 + 64, 64), 64), columns(k)] = high
+                put(fb[k], xl, k, 0).start()
 
             @pl.when(xl != OWNER[k])
             def _():
-                fb[k][0:64] = low
-                fb[k][64:128] = high
                 swap[k].start()
 
-    def columns(k):
-        return slice(STARTS[k] % 1024, STARTS[k] % 1024 + WIDTHS[k])
+    def put(src, block, k, n):
+        rows = pl.ds(pl.multiple_of(block * 128, 128), 128)
+        first = STARTS[k] % 1024
+        return pltpu.make_async_copy(src, out.at[rows, first:first + WIDTHS[k]], os.at[k, n])
 
     def conclude():
-        for k in last_chunks:
-            @pl.when(xl == OWNER[k])
-            def _():
-                swap[k].wait_recv()
-                out[pl.ds(pl.multiple_of((1 - xl) * 128, 128), 128), columns(k)] = fr[k][...]
-
-            @pl.when(xl != OWNER[k])
-            def _():
-                swap[k].wait_send()
         for group in x_dy + z_h + z_dy[0] + z_dy[1] + x_h + x_f:
             for cpy in group:
                 cpy.wait_send()
         for k in range(NCH):
             for cpy in (core[k],) + y_a[k] + y_b[k]:
                 cpy.wait_send()
+        for k in last_chunks:
+            @pl.when(xl == OWNER[k])
+            def _():
+                swap[k].wait_recv()
+                put(fr[k], 1 - xl, k, 1).start()
+
+            @pl.when(xl != OWNER[k])
+            def _():
+                swap[k].wait_send()
+        for k in last_chunks:
+            @pl.when(xl == OWNER[k])
+            def _():
+                put(fb[k], xl, k, 0).wait()
+                put(fr[k], 1 - xl, k, 1).wait()
 
     scales = lax.dot_general(eye[0:TOK, 0:TOK], ds[...], NT, preferred_element_type=F32)
     first_half, last_chunks = {}, []
@@ -284,7 +291,7 @@
         kernel,
         out_shape=jax.ShapeDtypeStruct((256, 1024), BF16),
         in_specs=[anywhere] * 4,
-        out_specs=pl.BlockSpec(memory_space=pltpu.VMEM),
+        out_specs=anywhere,
         scratch_shapes=[
             pltpu.VMEM((TOK, 16384), BF16),
             pltpu.VMEM((TOK, 128), BF16),
@@ -312,6 +319,7 @@
             dma((NCH,)), dma((NCH,)),
             dma((NCH, 4)), dma((NCH, 4)),
             dma((NCH,)), dma((NCH,)),
+            dma((NCH, 2)),
         ],
         compiler_params=pltpu.CompilerParams(
             collective_id=0, has_side_effects=True, vmem_limit_bytes=60 * 1024 * 1024),

time: 103 us -> 103 us (level)
  no operation moved by 1% of the time
where the time goes in v4:
time: 103 us; the launch traced here: 102 us
  Pallas kernels  101 us (98%)
  local copies, waits for them, and re-layouts  1.87 us (2%)
    pallas_call x1, Pallas kernels, shards(): pl.pallas_call(kernel, out_shape=jax.ShapeDtypeStruct((256, 1024), BF16),...  101 us

profile of v4, /device:TPU:2, one launch (start us, length us, event | category | flops | bytes accessed | tf_op | source)
XLA Modules:
  0.0 102.4 jit_solution(2457204140809807608)
XLA Ops:
  0.0 100.5 %shard_map.46 = bf16[256,1024]{1,0:T(8,128)(2,1)} custom-call(bf16[48,16384]{1,0:T(8,128)(2,1)} %hv_hbm.1, bf16[48,128]{1,0:T(8,128)(2,1)} %hs_hbm.1, bf16[48,4096]{1,0:T(8,128)(2,1)} %dv_hbm.1, bf16[32,48]{1,0:T(8,128)(2,1)} %bitcast.1), custom_call_target="tpu_custom_call" | custom-call | tf_op jit(solution)/shard_map/pallas_call | solution.py:290
  100.5 1.9 %copy.6 = bf16[256,1024]{1,0:T(8,128)(2,1)} copy(bf16[256,1024]{1,0:T(8,128)(2,1)} %shard_map.46) | data formatting | bytes 1048576

commit v5 on v4

--- a/solution.py
+++ b/solution.py
@@ -20,17 +20,17 @@
 F32, BF16 = jnp.float32, jnp.bfloat16
 NT = (((1,), (1,)), ((), ()))
 ORDER = (
-    ("dy",), ("bar",), ("h", 0), ("x0",), ("h", 3), ("r", 0), ("s", 0, 0), ("h", 1), ("r", 3), ("h", 2),
-    ("s", 0, 1), ("f", 0), ("f", 3), ("r", 1), ("s", 1, 0), ("s", 0, 2), ("r", 2), ("s", 1, 1), ("f", 1),
-    ("s", 0, 3), ("s", 1, 2), ("f", 2), ("h", 4), ("q", 0), ("P", 0, 1), ("P", 0, 3), ("P", 0, 0), ("s", 1, 3),
-    ("P", 0, 2), ("A", 0, 1), ("A", 0, 0), ("h", 6), ("h", 5), ("r", 4), ("A", 0, 3), ("A", 0, 2), ("q", 1),
-    ("B", 0, 3), ("r", 6), ("P", 1, 1), ("P", 1, 0), ("B", 0, 2), ("f", 4), ("B", 0, 1), ("P", 1, 3), ("A", 1, 1),
-    ("r", 5), ("P", 1, 2), ("A", 1, 3), ("f", 6), ("P", 0, 4), ("B", 1, 1), ("E", 0, 3), ("A", 1, 2), ("f", 5),
-    ("P", 1, 4), ("B", 1, 3), ("A", 0, 4), ("A", 1, 0), ("P", 1, 6), ("P", 0, 6), ("A", 1, 4), ("B", 1, 2),
-    ("P", 0, 5), ("P", 1, 5), ("E", 1, 1), ("A", 1, 6), ("A", 0, 6), ("E", 0, 2), ("A", 0, 5), ("A", 1, 5),
-    ("B", 1, 4), ("E", 1, 3), ("E", 0, 1), ("B", 0, 4), ("B", 1, 6), ("B", 1, 0), ("B", 0, 0), ("B", 0, 6),
-    ("B", 0, 5), ("E", 1, 2), ("B", 1, 5), ("E", 1, 4), ("E", 0, 4), ("E", 1, 6), ("E", 1, 0), ("E", 0, 0),
-    ("E", 0, 6), ("E", 0, 5), ("E", 1, 5), ("END",),
+    ("dy",), ("bar",), ("x0",), ("h", 0), ("h", 2), ("s", 0, 0), ("h", 1), ("h", 3), ("r", 2), ("r", 0), ("f", 2),
+    ("f", 0), ("r", 1), ("s", 0, 1), ("s", 1, 0), ("r", 3), ("s", 0, 2), ("f", 1), ("s", 1, 1), ("s", 0, 3),
+    ("s", 1, 2), ("h", 4), ("f", 3), ("q", 0), ("P", 0, 2), ("P", 0, 1), ("P", 0, 3), ("s", 1, 3), ("A", 0, 2),
+    ("A", 0, 1), ("h", 6), ("P", 0, 0), ("h", 5), ("r", 4), ("A", 0, 0), ("B", 0, 2), ("A", 0, 3), ("q", 1),
+    ("B", 0, 1), ("r", 6), ("P", 1, 0), ("P", 1, 3), ("f", 4), ("B", 0, 3), ("P", 1, 2), ("r", 5), ("A", 1, 0),
+    ("A", 1, 3), ("P", 1, 1), ("f", 6), ("A", 1, 2), ("P", 1, 4), ("P", 0, 4), ("A", 1, 1), ("f", 5), ("B", 1, 3),
+    ("A", 1, 4), ("B", 0, 0), ("B", 1, 2), ("P", 1, 6), ("P", 0, 6), ("A", 0, 4), ("B", 1, 1), ("P", 1, 5),
+    ("P", 0, 5), ("E", 0, 3), ("A", 1, 6), ("A", 0, 6), ("B", 1, 0), ("E", 0, 1), ("A", 1, 5), ("E", 0, 2),
+    ("A", 0, 5), ("B", 1, 4), ("E", 1, 3), ("B", 0, 4), ("E", 1, 1), ("E", 1, 2), ("B", 1, 6), ("E", 1, 0),
+    ("B", 0, 6), ("B", 1, 5), ("B", 0, 5), ("E", 1, 4), ("E", 0, 0), ("E", 1, 6), ("E", 0, 4), ("E", 0, 6),
+    ("E", 1, 5), ("E", 0, 5), ("END",),
 )
 
 

time: 103 us -> 102 us (level)
  no operation moved by 1% of the time
where the time goes in v5:
time: 102 us
  Pallas kernels  100 us (98%)
  local copies, waits for them, and re-layouts  1.87 us (2%)
    pallas_call x1, Pallas kernels, shards(): pl.pallas_call(kernel, out_shape=jax.ShapeDtypeStruct((256, 1024), BF16),...  100 us

profile of v5, /device:TPU:2, one launch (start us, length us, event | category | flops | bytes accessed | tf_op | source)
XLA Modules:
  0.0 102.2 jit_solution(4411728317017835789)
XLA Ops:
  0.0 100.4 %shard_map.46 = bf16[256,1024]{1,0:T(8,128)(2,1)} custom-call(bf16[48,16384]{1,0:T(8,128)(2,1)} %hv_hbm.1, bf16[48,128]{1,0:T(8,128)(2,1)} %hs_hbm.1, bf16[48,4096]{1,0:T(8,128)(2,1)} %dv_hbm.1, bf16[32,48]{1,0:T(8,128)(2,1)} %bitcast.1), custom_call_target="tpu_custom_call" | custom-call | tf_op jit(solution)/shard_map/pallas_call | solution.py:290
  100.4 1.9 %copy.6 = bf16[256,1024]{1,0:T(8,128)(2,1)} copy(bf16[256,1024]{1,0:T(8,128)(2,1)} %shard_map.46) | data formatting | bytes 1048576
